TPU v7x, 32 devices: a whole 2x2x4 slice. The times are simulated.
32 devices in a mesh: rows: 8 (over y, x, core), grp: 4 (over z).
Axes of the slice: x: 2, y: 2, z: 4, core: 2. Of those that a mesh axis runs over, the one named last changes fastest.
Arguments:
- pivot_columns: bfloat16 [32, 10240, 256], P('rows', 'grp'), may hold values from -6 to 6
- previous: bfloat16 [32, 10240, 512], P('rows', 'grp'), may hold values from -0.59765625 to 0.59765625
- pivots: int32 [256], replicated, may hold values from 0 to 327679, as said below
- pivot_inverse: bfloat16 [256, 256], replicated, may hold values from -0.4 to 1.5
- orbitals: bfloat16 [10240, 1024], P('grp'), may hold values from -0.0625 to 0.0625
- slab_orbitals: bfloat16 [32, 1024], replicated, may hold values from -1 to 1
Outputs:
- new_vectors: bfloat16 [32, 10240, 256], P('rows', 'grp')
- mo_block: bfloat16 [256, 1024, 1024], P('rows', None, 'grp')
Inputs may be any that keep to these rules, and one draw needn't show every extreme that they name: `pivots`: distinct entries.
All inputs are finite; a program needn't handle non-finite values.
Results may differ from a plain program's by a relative error of at most 0.0038.
The roundings to bfloat16 on the way count: a program that leaves them out, or rounds other values in their place, can miss the bound.
Values may be sent and summed in bfloat16 or wider, within the bound.
A program may use at most 128 MiB of HBM per device.

v0:
```python
import jax
import jax.numpy as jnp
from jax import lax
from jax.sharding import PartitionSpec as P

NBAS = 10240


def per_device(pivot_columns, previous, pivots, pivot_inverse, orbitals, slab_orbitals):
    mu_dev, nu_dev, prev_count = previous.shape
    pivot_count = pivot_columns.shape[2]
    row_index = lax.axis_index("rows")
    grp_index = lax.axis_index("grp")
    first_local = pivots // NBAS - row_index * mu_dev
    second_local = pivots % NBAS - grp_index * nu_dev
    owned = (
        (first_local >= 0) & (first_local < mu_dev) & (second_local >= 0) & (second_local < nu_dev)
    )
    local_row = jnp.where(owned, first_local * nu_dev + second_local, 0)
    flat_prev = previous.reshape(mu_dev * nu_dev, prev_count)
    picked = jnp.where(
        owned[:, None], jnp.take(flat_prev, local_row, axis=0).astype(jnp.float32), 0.0
    )
    pivot_rows = lax.psum(picked, ("rows", "grp")).astype(jnp.bfloat16)
    correction = jnp.dot(flat_prev, pivot_rows.T, preferred_element_type=jnp.float32)
    flat_columns = pivot_columns.reshape(mu_dev * nu_dev, pivot_count)
    residual_columns = (flat_columns.astype(jnp.float32) - correction).astype(jnp.bfloat16)
    upper = jnp.triu(pivot_inverse)
    new_flat = jnp.dot(residual_columns, upper, preferred_element_type=jnp.float32).astype(
        jnp.bfloat16
    )
    new_vectors = new_flat.reshape(mu_dev, nu_dev, pivot_count)
    half = lax.psum_scatter(
        jnp.einsum("nj,mnp->jmp", orbitals, new_vectors, preferred_element_type=jnp.float32),
        "grp",
        scatter_dimension=0,
        tiled=True,
    ).astype(jnp.bfloat16)
    summed = jnp.einsum(
        "mi,jmp->pij",
        slab_orbitals,
        lax.all_to_all(half, "rows", split_axis=2, concat_axis=1, tiled=True),
        preferred_element_type=jnp.float32,
    )
    mo_block = summed.astype(jnp.bfloat16)
    return (new_vectors, mo_block)


def solution(mesh):
    in_specs = (P("rows", "grp", None), P("rows", "grp", None), P(), P(), P("grp", None), P())
    out_specs = (P("rows", "grp", None), P("rows", None, "grp"))
    return jax.shard_map(
        per_device, mesh=mesh, in_specs=in_specs, out_specs=out_specs, check_vma=False
    )
```

profile of v0, /device:TPU:0, one launch (start us, length us, event | category | flops | bytes accessed | tf_op | source)
XLA Modules:
  0.0 210.1 jit_solution(867711834112606244)
XLA Ops:
  7.2 0.0 copy-start
  7.2 0.0 reduce-scatter.2.cloned.1.call-start
  7.2 0.7 compare_and_fusion
  8.0 6.5 %gather_fusion = bf16[256,512]{1,0:T(8,128)(2,1)S(1)} fusion(bf16[10240,512]{1,0:T(8,128)(2,1)} %bitcast.36, s32[1024]{0:T(1024)S(1)} %pad_clamp_fusion), kind=kCustom, calls=%fused_computation | custom fusion | bytes 525312 | tf_op jit(solution)/shard_map/jit(_take)/gather | solution.py:22
  14.5 0.1 convert_select_fusion
  14.7 47.2 %all-reduce.1 = bf16[256,512]{1,0:T(8,128)(2,1)S(1)} all-reduce(f32[256,512]{1,0:T(8,128)S(1)} %convert_select_fusion), channel_id=1, replica_groups=mesh['rows'=8,'grp'=4] {'rows','grp'}, use_global_device_ids=true, to_apply=%region_0.1 | all-reduce | flops 131072 | bytes 786432 | tf_op jit(solution)/shard_map/psum | solution.py:24
  61.9 9.6 %convolution_convert_fusion = bf16[10240,256]{1,0:T(8,128)(2,1)} fusion(bf16[10240,512]{1,0:T(8,128)(2,1)} %bitcast.37, bf16[10240,256]{1,0:T(8,128)(2,1)} %bitcast.38, bf16[256,512]{1,0:T(8,128)(2,1)S(1)} %all-reduce.1, bf16[256,256]{1,0:T(8,128)(2,1)} %param.9, s32[256]{0:T(256)S(1)} %iota_add_fusion), kind=kOutput, calls=%fused_computation.5 | convolution fusion | flops 4037148672 | bytes 21365760 | tf_op jit(solution)/shard_map/dot_general | solution.py:29
  71.5 10.4 %fusion.4 = f32[1024,4,256]{0,2,1:T(8,128)} fusion(bf16[4,2560,256]{2,1,0:T(8,128)(2,1)} %bitcast.39, bf16[2560,1024]{1,0:T(8,128)(2,1)} %param.10), kind=kOutput, calls=%fused_computation.8 | convolution fusion | flops 5368709120 | bytes 14680064 | tf_op jit(solution)/shard_map/nj,mnp->jmp/dot_general | solution.py:34
  81.9 0.0 reduce-scatter.2.cloned.1.call-update
  81.9 75.4 %reduce-scatter.2.cloned.1.call-done = f32[256,4,256]{0,2,1:T(8,128)} async-done(((f32[1024,4,256]{0,2,1:T(8,128)}), f32[256,4,256]{0,2,1:T(8,128)}) %reduce-scatter.2.cloned.1.call-update) | async-done | bytes 1048592 | tf_op jit(solution)/shard_map/reduce_scatter | solution.py:33
  157.3 1.3 convert_element_type.33
  158.6 0.4 copy.12
  159.0 13.2 %all_to_all.18 = bf16[256,4,256]{0,1,2:T(4,128)(2,1)S(1)} all-to-all(bf16[256,4,256]{0,1,2:T(4,128)(2,1)S(1)} %copy.12), channel_id=1, replica_groups=mesh['rows'=8,'grp'=4] {'rows'}, dimensions={2} | all-to-all | bytes 1048576 | tf_op jit(solution)/shard_map/all_to_all | solution.py:42
  172.2 0.3 copy.17
  172.5 0.1 all_to_all.16
  172.6 0.0 copy-done
  172.6 8.1 %convert_bitcast_fusion = bf16[32,1024,256]{1,2,0:T(8,128)(2,1)} fusion(bf16[256,32,32]{0,1,2:T(8,128)(2,1)S(1)} %all_to_all.16, bf16[32,1024]{1,0:T(8,128)(2,1)S(1)} %copy-done), kind=kOutput, calls=%fused_computation.1 | convolution fusion | flops 545259520 | bytes 17367040 | tf_op jit(solution)/shard_map/mi,jmp->pij/dot_general | solution.py:39
  180.8 0.0 copy-start.1
  180.8 22.5 %copy.14 = bf16[32,1024,256]{2,1,0:T(8,128)(2,1)} copy(bf16[32,1024,256]{1,2,0:T(8,128)(2,1)} %convert_bitcast_fusion) | data formatting | bytes 33554432
  203.2 0.0 copy-done.1
  (2 shorter events, 0.0 us)
Async XLA Ops:
  7.2 165.5 %copy-start = (bf16[32,1024]{1,0:T(8,128)(2,1)S(1)}, bf16[32,1024]{1,0:T(8,128)(2,1)}, u32[]{:S(2)}) copy-start(bf16[32,1024]{1,0:T(8,128)(2,1)} %param.11) | copy-start | bytes 196612
  7.2 150.1 %reduce-scatter.2.cloned.1.call-start = ((), (), s32[]{:S(2)}) async-start(), calls=%async_computation.2 | async-start | bytes 5242880 | tf_op jit(solution)/shard_map/reduce_scatter | solution.py:33
  180.8 22.5 %copy-start.1 = (bf16[32,1024]{1,0:T(8,128)(2,1)S(1)}, bf16[32,1024]{1,0:T(8,128)(2,1)}, u32[]{:S(2)}) copy-start(bf16[32,1024]{1,0:T(8,128)(2,1)} %param.11) | copy-start | bytes 196612
Sparse Core Ops, SparseCore 0:
  82.0 75.2 reduce-scatter.1
where the time goes:
time: 211 us; the launch traced here: 210 us
  waiting for transfers between devices  75.4 us (36%)
  blocking collectives  60.4 us (29%)
  local copies, waits for them, and re-layouts  29.8 us (14%)
  matrix products  28.1 us (13%)
  between operations  14.1 us (7%)
  other arithmetic  2.13 us (1%)
    reduce_scatter x1, waiting for transfers between devices, per_device(): lax.psum_scatter(jnp.einsum('nj,mnp->jmp', orbitals, new_vectors, preferr...  75.4 us
    psum x1, blocking collectives, per_device(): pivot_rows = lax.psum(picked, ('rows', 'grp')).astype(jnp.bfloat16)  47.2 us
    unnamed x5, local copies, waits for them, and re-layouts  22.5 us
    all_to_all x1, blocking collectives, per_device(): lax.all_to_all(half, 'rows', split_axis=2, concat_axis=1, tiled=True)  13.2 us
    dot_general x1, matrix products, per_device(): jnp.einsum('nj,mnp->jmp', orbitals, new_vectors, preferred_element_type=j...  10.4 us
    dot_general x1, matrix products, per_device(): jnp.dot(residual_columns, upper, preferred_element_type=jnp.float32)  9.58 us
    dot_general x1, matrix products, per_device(): jnp.einsum('mi,jmp->pij', slab_orbitals, lax.all_to_all(half, 'rows', spl...  8.14 us
    gather x1, local copies, waits for them, and re-layouts, per_device(): jnp.take(flat_prev, local_row, axis=0).astype(jnp.float32)  6.54 us
  transfers between devices with their start and end apart: 1, of which 1 were waited for; matrix products, arithmetic and copies ran while one was open for 0% of the time, Pallas kernels for 0%

commit v1 on v0

--- a/solution.py
+++ b/solution.py
@@ -4,6 +4,7 @@
 from jax.sharding import PartitionSpec as P
 
 NBAS = 10240
+cut_copies_now = lambda incoming_x: lax.psum(lax.psum(incoming_x, axis_name="grp"), "rows")
 
 
 def per_device(pivot_columns, previous, pivots, pivot_inverse, orbitals, slab_orbitals):
@@ -21,7 +22,7 @@
     picked = jnp.where(
         owned[:, None], jnp.take(flat_prev, local_row, axis=0).astype(jnp.float32), 0.0
     )
-    pivot_rows = lax.psum(picked, ("rows", "grp")).astype(jnp.bfloat16)
+    pivot_rows = cut_copies_now(picked).astype(jnp.bfloat16)
     correction = jnp.dot(flat_prev, pivot_rows.T, preferred_element_type=jnp.float32)
     flat_columns = pivot_columns.reshape(mu_dev * nu_dev, pivot_count)
     residual_columns = (flat_columns.astype(jnp.float32) - correction).astype(jnp.bfloat16)

time: 211 us -> 236 us (1.12)
  waiting for transfers between devices: 75.4 us -> 116 us
  blocking collectives: 60.4 us -> 44.1 us
    psum x0 -> x1, waiting for transfers between devices: none -> 41.3 us  [lax.psum(incoming_x, axis_name='grp')]
    psum x1, blocking collectives: 47.2 us -> 30.9 us  [lax.psum(lax.psum(incoming_x, axis_name='grp'), 'rows')]
  transfers between devices with their start and end apart: 1 -> 2, of which waited for: 1 -> 2; matrix products, arithmetic and copies ran while one was open for 0% -> 0% of each run, Pallas kernels for 0% -> 0%
where the time goes in v1:
time: 236 us; the launch traced here: 235 us
  waiting for transfers between devices  116 us (49%)
  blocking collectives  44.1 us (19%)
  local copies, waits for them, and re-layouts  29.8 us (13%)
  matrix products  28.1 us (12%)
  between operations  14.1 us (6%)
  other arithmetic  2.92 us (1%)
    reduce_scatter x1, waiting for transfers between devices, per_device(): lax.psum_scatter(jnp.einsum('nj,mnp->jmp', orbitals, new_vectors, preferr...  74.3 us
    psum x1, waiting for transfers between devices, lax.psum(incoming_x, axis_name='grp')  41.3 us
    psum x1, blocking collectives, lax.psum(lax.psum(incoming_x, axis_name='grp'), 'rows')  30.9 us
    unnamed x5, local copies, waits for them, and re-layouts  22.5 us
    all_to_all x1, blocking collectives, per_device(): lax.all_to_all(half, 'rows', split_axis=2, concat_axis=1, tiled=True)  13.2 us
    dot_general x1, matrix products, per_device(): jnp.einsum('nj,mnp->jmp', orbitals, new_vectors, preferred_element_type=j...  10.4 us
    dot_general x1, matrix products, per_device(): jnp.dot(residual_columns, upper, preferred_element_type=jnp.float32)  9.56 us
    dot_general x1, matrix products, per_device(): jnp.einsum('mi,jmp->pij', slab_orbitals, lax.all_to_all(half, 'rows', spl...  8.14 us
  transfers between devices with their start and end apart: 2, of which 2 were waited for; matrix products, arithmetic and copies ran while one was open for 0% of the time, Pallas kernels for 0%

profile of v1, /device:TPU:0, one launch (start us, length us, event | category | flops | bytes accessed | tf_op | source)
XLA Modules:
  0.0 234.8 jit_solution(2680704401957630629)
XLA Ops:
  7.2 0.0 copy-start
  7.2 0.0 all-reduce.3.cloned.1.call-start
  7.2 0.7 compare_and_fusion
  8.0 6.5 %gather_fusion = bf16[256,512]{1,0:T(8,128)(2,1)S(1)} fusion(bf16[10240,512]{1,0:T(8,128)(2,1)} %bitcast.36, s32[1024]{0:T(1024)S(1)} %pad_clamp_fusion), kind=kCustom, calls=%fused_computation | custom fusion | bytes 525312 | tf_op jit(solution)/shard_map/jit(_take)/gather | solution.py:23
  14.5 0.9 convert_select_fusion
  15.4 0.0 all-reduce.3.cloned.1.call-update
  15.5 0.0 reduce-scatter.2.cloned.1.call-start
  15.5 41.3 %all-reduce.3.cloned.1.call-done = f32[256,512]{1,0:T(8,128)} async-done(((f32[256,512]{1,0:T(8,128)}), f32[256,512]{1,0:T(8,128)}) %all-reduce.3.cloned.1.call-update) | async-done | bytes 524304 | tf_op jit(solution)/shard_map/psum | solution.py:7
  56.8 30.9 %all-reduce.4 = bf16[256,512]{1,0:T(8,128)(2,1)S(1)} all-reduce(f32[256,512]{1,0:T(8,128)} %all-reduce.3.cloned.1.call-done), channel_id=1, replica_groups=mesh['rows'=8,'grp'=4] {'rows'}, use_global_device_ids=true, to_apply=%region_1.2 | all-reduce | flops 131072 | bytes 786432 | tf_op jit(solution)/shard_map/psum | solution.py:7
  87.8 9.6 %convolution_convert_fusion = bf16[10240,256]{1,0:T(8,128)(2,1)} fusion(bf16[10240,512]{1,0:T(8,128)(2,1)} %bitcast.37, bf16[10240,256]{1,0:T(8,128)(2,1)} %bitcast.38, bf16[256,512]{1,0:T(8,128)(2,1)S(1)} %all-reduce.4, bf16[256,256]{1,0:T(8,128)(2,1)} %param.9, s32[256]{0:T(256)S(1)} %iota_add_fusion), kind=kOutput, calls=%fused_computation.5 | convolution fusion | flops 4037148672 | bytes 21365760 | tf_op jit(solution)/shard_map/dot_general | solution.py:30
  97.4 10.4 %fusion.4 = f32[1024,4,256]{0,2,1:T(8,128)} fusion(bf16[4,2560,256]{2,1,0:T(8,128)(2,1)} %bitcast.39, bf16[2560,1024]{1,0:T(8,128)(2,1)} %param.10), kind=kOutput, calls=%fused_computation.8 | convolution fusion | flops 5368709120 | bytes 14680064 | tf_op jit(solution)/shard_map/nj,mnp->jmp/dot_general | solution.py:35
  107.8 0.0 reduce-scatter.2.cloned.1.call-update
  107.8 74.3 %reduce-scatter.2.cloned.1.call-done = f32[256,4,256]{0,2,1:T(8,128)} async-done(((f32[1024,4,256]{0,2,1:T(8,128)}), f32[256,4,256]{0,2,1:T(8,128)}) %reduce-scatter.2.cloned.1.call-update) | async-done | bytes 1048592 | tf_op jit(solution)/shard_map/reduce_scatter | solution.py:34
  182.1 1.3 convert_element_type.33
  183.4 0.4 copy.12
  183.8 13.2 %all_to_all.18 = bf16[256,4,256]{0,1,2:T(4,128)(2,1)S(1)} all-to-all(bf16[256,4,256]{0,1,2:T(4,128)(2,1)S(1)} %copy.12), channel_id=1, replica_groups=mesh['rows'=8,'grp'=4] {'rows'}, dimensions={2} | all-to-all | bytes 1048576 | tf_op jit(solution)/shard_map/all_to_all | solution.py:43
  197.0 0.3 copy.17
  197.3 0.1 all_to_all.16
  197.4 0.0 copy-done
  197.4 8.1 %convert_bitcast_fusion = bf16[32,1024,256]{1,2,0:T(8,128)(2,1)} fusion(bf16[256,32,32]{0,1,2:T(8,128)(2,1)S(1)} %all_to_all.16, bf16[32,1024]{1,0:T(8,128)(2,1)S(1)} %copy-done), kind=kOutput, calls=%fused_computation.1 | convolution fusion | flops 545259520 | bytes 17367040 | tf_op jit(solution)/shard_map/mi,jmp->pij/dot_general | solution.py:40
  205.5 0.0 copy-start.1
  205.5 22.5 %copy.14 = bf16[32,1024,256]{2,1,0:T(8,128)(2,1)} copy(bf16[32,1024,256]{1,2,0:T(8,128)(2,1)} %convert_bitcast_fusion) | data formatting | bytes 33554432
  228.0 0.0 copy-done.1
  (2 shorter events, 0.0 us)
Async XLA Ops:
  7.2 190.2 %copy-start = (bf16[32,1024]{1,0:T(8,128)(2,1)S(1)}, bf16[32,1024]{1,0:T(8,128)(2,1)}, u32[]{:S(2)}) copy-start(bf16[32,1024]{1,0:T(8,128)(2,1)} %param.11) | copy-start | bytes 196612
  7.2 49.7 %all-reduce.3.cloned.1.call-start = ((), (), s32[]{:S(2)}) async-start(), calls=%async_computation.2 | async-start | bytes 1048576 | tf_op jit(solution)/shard_map/psum | solution.py:7
  15.5 166.7 %reduce-scatter.2.cloned.1.call-start = ((), (), s32[]{:S(2)}) async-start(), calls=%async_computation.3 | async-start | bytes 5242880 | tf_op jit(solution)/shard_map/reduce_scatter | solution.py:34
  205.5 22.5 %copy-start.1 = (bf16[32,1024]{1,0:T(8,128)(2,1)S(1)}, bf16[32,1024]{1,0:T(8,128)(2,1)}, u32[]{:S(2)}) copy-start(bf16[32,1024]{1,0:T(8,128)(2,1)} %param.11) | copy-start | bytes 196612
Sparse Core Ops, SparseCore 0:
  15.6 41.2 all-reduce.2
  107.9 74.1 reduce-scatter.1
